TPU v7x, 32 devices: a whole 2x2x4 slice. The times are simulated.
32 devices in a mesh: row: 4 (over x, core), col: 8 (over z, y).
Axes of the slice: x: 2, y: 2, z: 4, core: 2. Of those that a mesh axis runs over, the one named last changes fastest.
Arguments:
- ancestor_inverse: bfloat16 [24576, 24576], P('row', 'col'), may hold values from -0.0390625 to 0.0390625
- panels: bfloat16 [24576, 3, 512], P(('row', 'col')), may hold values from -1.1953125 to 1.1953125
- diag_inverse: float32 [3, 512, 512], replicated, may hold values from -6 to 6
- tile_mask: int32 [3, 192], replicated, may hold values 0 or 1
Outputs:
- off_diagonal: float32 [24576, 3, 512], P(('row', 'col'))
- diagonal: float32 [3, 512, 512], replicated
All inputs are finite; a program needn't handle non-finite values.
Results may differ from a plain program's by a relative error of at most 0.0003.
Values may be sent and summed in bfloat16 or wider, within the bound.
A program may use at most 192 MiB of HBM per device.

v0:
```python
import jax
import jax.numpy as jnp
from jax import lax
from jax.sharding import PartitionSpec as P


def exchange(partial, axis):
    count = lax.axis_size(axis)
    rows, width = partial.shape
    return lax.psum_scatter(partial, axis, scatter_dimension=0, tiled=True)


def body(ancestor_inverse, panels, diag_inverse, tile_mask):
    row_count = lax.axis_size("row")
    col_count = lax.axis_size("col")
    span = lax.axis_index("row") * col_count + lax.axis_index("col")
    kept_rows = panels.shape[0]
    panel_count = panels.shape[1]
    tile = kept_rows * row_count * col_count // tile_mask.shape[1]
    full_mask = jnp.repeat(tile_mask, tile, axis=1).astype(jnp.bfloat16)
    own_mask = lax.dynamic_slice_in_dim(full_mask, span * kept_rows, kept_rows, 1)
    moves = [
        (index, index % row_count * col_count + index // row_count)
        for index in range(row_count * col_count)
    ]
    masked = [panels[:, p, :] * own_mask[p][:, None] for p in range(panel_count)]
    sent = [lax.ppermute(block, ("row", "col"), moves) for block in masked]
    sides = [lax.all_gather(block, "row", axis=0, tiled=True) for block in sent]
    results, parts = ([], [])
    for p in range(panel_count):
        partial = jnp.dot(ancestor_inverse, sides[p], preferred_element_type=jnp.float32)
        summed = -exchange(partial, "col")
        results.append(summed)
        parts.append(
            lax.dot_general(
                masked[p].astype(jnp.float32),
                summed,
                (((0,), (0,)), ((), ())),
                precision=lax.Precision.HIGHEST,
            )
        )
    off_diagonal = jnp.stack(results, axis=1)
    schur = lax.psum(jnp.stack(parts), ("row", "col"))
    return (off_diagonal, diag_inverse - schur)


def solution(mesh):
    return jax.shard_map(
        body,
        mesh=mesh,
        in_specs=(P("row", "col"), P(("row", "col"), None, None), P(), P()),
        out_specs=(P(("row", "col"), None, None), P()),
        check_vma=False,
    )
```

profile of v0, /device:TPU:0, one launch (start us, length us, event | category | flops | bytes accessed | tf_op | source)
XLA Modules:
  0.0 952.1 jit_solution(13903537531053839367)
XLA Ops:
  7.2 0.7 convert_element_type.10
  8.3 2.0 bitcast_multiply_fusion.2
  10.3 1.6 collective-permute-start.2
  12.0 1.6 collective-permute-start
  13.6 1.5 collective-permute-start.1
  15.2 86.4 %all-gather.8.cloned.1.call-done = bf16[3072,512]{1,0:T(8,128)(2,1)} async-done(((bf16[768,512]{1,0:T(8,128)(2,1)}), bf16[3072,512]{1,0:T(8,128)(2,1)}) %all-gather.8.cloned.1.call-update) | async-done | bytes 3145744 | tf_op jit(solution)/shard_map/all_gather | solution.py:28
  101.6 27.8 %convolution_bitcast_fusion = f32[6144,512]{0,1:T(8,128)} fusion(bf16[3072,512]{1,0:T(8,128)(2,1)} %all-gather.8.cloned.1.call-done, bf16[6144,3072]{1,0:T(8,128)(2,1)} %param.4), kind=kOutput, calls=%fused_computation | convolution fusion | flops 19327352832 | bytes 53477376 | tf_op jit(solution)/shard_map/dot_general | solution.py:31
  129.7 5.6 all-gather.4.cloned.1.call-done
  135.3 27.7 %convolution_bitcast_fusion.2 = f32[6144,512]{0,1:T(8,128)} fusion(bf16[3072,512]{1,0:T(8,128)(2,1)} %all-gather.4.cloned.1.call-done, bf16[6144,3072]{1,0:T(8,128)(2,1)} %param.4), kind=kOutput, calls=%fused_computation.2 | convolution fusion | flops 19327352832 | bytes 53477376 | tf_op jit(solution)/shard_map/dot_general | solution.py:31
  163.3 3.3 all-gather.6.cloned.1.call-done
  166.6 27.7 %convolution_bitcast_fusion.1 = f32[6144,512]{0,1:T(8,128)} fusion(bf16[3072,512]{1,0:T(8,128)(2,1)} %all-gather.6.cloned.1.call-done, bf16[6144,3072]{1,0:T(8,128)(2,1)} %param.4), kind=kOutput, calls=%fused_computation.1 | convolution fusion | flops 19327352832 | bytes 53477376 | tf_op jit(solution)/shard_map/dot_general | solution.py:31
  194.6 182.9 %reduce-scatter.8.cloned.1.call-done = f32[768,512]{0,1:T(8,128)} async-done(((f32[6144,512]{0,1:T(8,128)}), f32[768,512]{0,1:T(8,128)}) %reduce-scatter.8.cloned.1.call-update) | async-done | bytes 1572880 | tf_op jit(solution)/shard_map/reduce_scatter | solution.py:10
  377.5 3.1 fusion.12
  380.7 206.9 %reduce-scatter.4.cloned.1.call-done = f32[768,512]{0,1:T(8,128)} async-done(((f32[6144,512]{0,1:T(8,128)}), f32[768,512]{0,1:T(8,128)}) %reduce-scatter.4.cloned.1.call-update) | async-done | bytes 1572880 | tf_op jit(solution)/shard_map/reduce_scatter | solution.py:10
  587.6 3.4 fusion.6
  590.9 206.7 %reduce-scatter.6.cloned.1.call-done = f32[768,512]{0,1:T(8,128)} async-done(((f32[6144,512]{0,1:T(8,128)}), f32[768,512]{0,1:T(8,128)}) %reduce-scatter.6.cloned.1.call-update) | async-done | bytes 1572880 | tf_op jit(solution)/shard_map/reduce_scatter | solution.py:10
  797.6 3.1 fusion.9
  800.7 2.0 pad_maximum_fusion.1
  802.7 1.4 copy-done
  804.7 0.9 copy-done.1
  805.8 2.4 pad_maximum_fusion
  808.2 6.2 copy.6
  814.4 126.5 %all-reduce.2.cloned.1.call-done = f32[3,512,512]{2,1,0:T(8,128)} async-done(((f32[3,512,512]{2,1,0:T(8,128)}), f32[3,512,512]{2,1,0:T(8,128)}) %all-reduce.2.cloned.1.call-update) | async-done | bytes 3145744 | tf_op jit(solution)/shard_map/psum | solution.py:43
  941.0 4.3 sub.3
  (31 shorter events, 2.1 us)
Async XLA Ops:
  7.2 94.5 %all-gather.8.cloned.1.call-start = ((), (), s32[]{:S(2)}) async-start(), calls=%async_computation.7 | async-start | bytes 3932160 | tf_op jit(solution)/shard_map/all_gather | solution.py:28
  10.3 119.1 %copy-start.4 = (bf16[768,512]{1,0:T(8,128)(2,1)}, bf16[768,512]{1,0:T(8,128)(2,1)S(1)}, u32[]{:S(2)}) copy-start(bf16[768,512]{1,0:T(8,128)(2,1)S(1)} %get-tuple-element.7) | copy-start | bytes 2359300
  10.3 1.6 collective-permute-start.2
  11.9 123.4 %all-gather.4.cloned.1.call-start = ((), (), s32[]{:S(2)}) async-start(), calls=%async_computation.3 | async-start | bytes 3932160 | tf_op jit(solution)/shard_map/all_gather | solution.py:28
  12.0 1.6 collective-permute-start
  13.6 153.1 %all-gather.6.cloned.1.call-start = ((), (), s32[]{:S(2)}) async-start(), calls=%async_computation.5 | async-start | bytes 3932160 | tf_op jit(solution)/shard_map/all_gather | solution.py:28
  13.6 1.5 collective-permute-start.1
  15.2 362.4 %reduce-scatter.8.cloned.1.call-start = ((), (), s32[]{:S(2)}) async-start(), calls=%async_computation.8 | async-start | bytes 14155776 | tf_op jit(solution)/shard_map/reduce_scatter | solution.py:10
  129.4 458.1 %reduce-scatter.4.cloned.1.call-start = ((), (), s32[]{:S(2)}) async-start(), calls=%async_computation.4 | async-start | bytes 14155776 | tf_op jit(solution)/shard_map/reduce_scatter | solution.py:10
  163.1 634.6 %reduce-scatter.6.cloned.1.call-start = ((), (), s32[]{:S(2)}) async-start(), calls=%async_computation.6 | async-start | bytes 14155776 | tf_op jit(solution)/shard_map/reduce_scatter | solution.py:10
  194.3 746.7 %all-reduce.2.cloned.1.call-start = ((), (), s32[]{:S(2)}) async-start(), calls=%async_computation.9 | async-start | bytes 6291456 | tf_op jit(solution)/shard_map/psum | solution.py:43
  802.7 1.4 copy-start
  802.7 1.9 copy-start.2
  804.1 1.5 copy-start.1
  808.2 132.8 %copy-start.3 = (f32[3,512,512]{2,1,0:T(8,128)S(1)}, f32[3,512,512]{2,1,0:T(8,128)}, u32[]{:S(2)}) copy-start(f32[3,512,512]{2,1,0:T(8,128)} %param.6) | copy-start | bytes 9437188
Sparse Core Ops, SparseCore 0:
  12.0 89.5 all-gather.7
  103.2 32.0 all-gather.3
  136.9 29.7 all-gather.5
  170.0 207.4 reduce-scatter.7
  381.0 206.5 reduce-scatter.3
  591.0 206.5 reduce-scatter.5
  803.7 137.2 all-reduce.1
where the time goes:
time: 953 us; the launch traced here: 952 us
  waiting for transfers between devices  818 us (86%)
  matrix products  92.8 us (10%)
  between operations  14.2 us (1%)
  other arithmetic  11.7 us (1%)
    reduce_scatter x3, waiting for transfers between devices, exchange(): return lax.psum_scatter(partial, axis, scatter_dimension=0, tiled=True)  597 us
    psum x1, waiting for transfers between devices, body(): schur = lax.psum(jnp.stack(parts), ('row', 'col'))  127 us
    all_gather x3, waiting for transfers between devices, body(): sides = [lax.all_gather(block, 'row', axis=0, tiled=True) for block in sent]  95.3 us
    dot_general x3, matrix products, body(): jnp.dot(ancestor_inverse, sides[p], preferred_element_type=jnp.float32)  83.2 us
  transfers between devices with their start and end apart: 10, of which 7 were waited for; matrix products, arithmetic and copies ran while one was open for 10% of the time, Pallas kernels for 0%

commit v1 on v0

--- a/solution.py
+++ b/solution.py
@@ -25,7 +25,12 @@
     ]
     masked = [panels[:, p, :] * own_mask[p][:, None] for p in range(panel_count)]
     sent = [lax.ppermute(block, ("row", "col"), moves) for block in masked]
-    sides = [lax.all_gather(block, "row", axis=0, tiled=True) for block in sent]
+    sides = [
+        jnp.concatenate(
+            lax.all_to_all(jnp.stack([block] * lax.axis_size("row")), "row", 0, 0), axis=0
+        )
+        for block in sent
+    ]
     results, parts = ([], [])
     for p in range(panel_count):
         partial = jnp.dot(ancestor_inverse, sides[p], preferred_element_type=jnp.float32)

time: 953 us -> 943 us (0.990)
  waiting for transfers between devices: 818 us -> 540 us
  blocking collectives: 0 us -> 270 us
    all_to_all x0 -> x3, blocking collectives: none -> 270 us  [body(): lax.all_to_all(jnp.stack([block] * lax.axis_size('row')), 'row', 0, 0)]
    reduce_scatter x3, waiting for transfers between devices: 597 us -> 414 us  [exchange(): return lax.psum_scatter(partial, axis, scatter_dimension=0, tiled=True)]
    all_gather x3 -> x0, waiting for transfers between devices: 95.3 us -> none  [body(): sides = [lax.all_gather(block, 'row', axis=0, tiled=True) for block in sent]]
  transfers between devices with their start and end apart: 10 -> 7, of which waited for: 7 -> 4; matrix products, arithmetic and copies ran while one was open for 10% -> 7% of each run, Pallas kernels for 0% -> 0%
where the time goes in v1:
time: 943 us; the launch traced here: 942 us
  waiting for transfers between devices  540 us (57%)
  blocking collectives  270 us (29%)
  matrix products  90.1 us (10%)
  between operations  13.9 us (1%)
  other arithmetic  12.8 us (1%)
  local copies, waits for them, and re-layouts  12.8 us (1%)
    reduce_scatter x3, waiting for transfers between devices, exchange(): return lax.psum_scatter(partial, axis, scatter_dimension=0, tiled=True)  414 us
    all_to_all x3, blocking collectives, body(): lax.all_to_all(jnp.stack([block] * lax.axis_size('row')), 'row', 0, 0)  270 us
    psum x1, waiting for transfers between devices, body(): schur = lax.psum(jnp.stack(parts), ('row', 'col'))  126 us
    dot_general x3, matrix products, body(): jnp.dot(ancestor_inverse, sides[p], preferred_element_type=jnp.float32)  80.5 us
  transfers between devices with their start and end apart: 7, of which 4 were waited for; matrix products, arithmetic and copies ran while one was open for 7% of the time, Pallas kernels for 0%

profile of v1, /device:TPU:0, one launch (start us, length us, event | category | flops | bytes accessed | tf_op | source)
XLA Modules:
  0.0 942.0 jit_solution(18227195926967831798)
XLA Ops:
  8.3 3.1 bitcast_multiply_fusion.2
  11.4 0.7 collective-permute-start.2
  12.6 62.3 %all_to_all.15 = bf16[4,768,512]{2,1,0:T(8,128)(2,1)S(1)} all-to-all(bf16[4,768,512]{2,1,0:T(8,128)(2,1)S(1)} %stack.49), channel_id=1, replica_groups=mesh['row'=4,'col'=8] {'row'}, dimensions={0} | all-to-all | bytes 6291456 | tf_op jit(solution)/shard_map/all_to_all | solution.py:30
  74.8 26.7 %convolution_bitcast_fusion = f32[6144,512]{0,1:T(8,128)} fusion(bf16[3072,512]{1,0:T(8,128)(2,1)S(1)} %bitcast.41, bf16[6144,3072]{1,0:T(8,128)(2,1)} %param.4), kind=kOutput, calls=%fused_computation | convolution fusion | flops 19327352832 | bytes 53477376 | tf_op jit(solution)/shard_map/dot_general | solution.py:36
  101.6 1.1 copy-done.6
  102.7 0.7 collective-permute-start
  103.6 95.1 %all_to_all.16 = bf16[4,768,512]{2,1,0:T(8,128)(2,1)S(1)} all-to-all(bf16[4,768,512]{2,1,0:T(8,128)(2,1)S(1)} %stack.22), channel_id=1, replica_groups=mesh['row'=4,'col'=8] {'row'}, dimensions={0} | all-to-all | bytes 6291456 | tf_op jit(solution)/shard_map/all_to_all | solution.py:30
  198.7 26.9 %convolution_bitcast_fusion.2 = f32[6144,512]{0,1:T(8,128)} fusion(bf16[3072,512]{1,0:T(8,128)(2,1)S(1)} %bitcast.42, bf16[6144,3072]{1,0:T(8,128)(2,1)} %param.4), kind=kOutput, calls=%fused_computation.2 | convolution fusion | flops 19327352832 | bytes 53477376 | tf_op jit(solution)/shard_map/dot_general | solution.py:36
  225.7 1.1 copy-done.4
  226.8 0.7 collective-permute-start.1
  227.8 112.4 %all_to_all.17 = bf16[4,768,512]{2,1,0:T(8,128)(2,1)S(1)} all-to-all(bf16[4,768,512]{2,1,0:T(8,128)(2,1)S(1)} %stack.47), channel_id=1, replica_groups=mesh['row'=4,'col'=8] {'row'}, dimensions={0} | all-to-all | bytes 6291456 | tf_op jit(solution)/shard_map/all_to_all | solution.py:30
  340.1 26.8 %convolution_bitcast_fusion.1 = f32[6144,512]{0,1:T(8,128)} fusion(bf16[3072,512]{1,0:T(8,128)(2,1)S(1)} %bitcast.43, bf16[6144,3072]{1,0:T(8,128)(2,1)} %param.4), kind=kOutput, calls=%fused_computation.1 | convolution fusion | flops 19327352832 | bytes 53477376 | tf_op jit(solution)/shard_map/dot_general | solution.py:36
  368.1 3.1 fusion.12
  371.2 206.6 %reduce-scatter.4.cloned.1.call-done = f32[768,512]{0,1:T(8,128)} async-done(((f32[6144,512]{0,1:T(8,128)}), f32[768,512]{0,1:T(8,128)}) %reduce-scatter.4.cloned.1.call-update) | async-done | bytes 1572880 | tf_op jit(solution)/shard_map/reduce_scatter | solution.py:10
  577.8 3.4 fusion.6
  581.2 206.8 %reduce-scatter.6.cloned.1.call-done = f32[768,512]{0,1:T(8,128)} async-done(((f32[6144,512]{0,1:T(8,128)}), f32[768,512]{0,1:T(8,128)}) %reduce-scatter.6.cloned.1.call-update) | async-done | bytes 1572880 | tf_op jit(solution)/shard_map/reduce_scatter | solution.py:10
  788.0 3.1 fusion.9
  791.1 2.0 pad_maximum_fusion.1
  793.1 1.4 copy-done
  795.1 0.9 copy-done.1
  796.1 2.4 pad_maximum_fusion
  798.6 6.2 copy.6
  804.8 126.4 %all-reduce.2.cloned.1.call-done = f32[3,512,512]{2,1,0:T(8,128)} async-done(((f32[3,512,512]{2,1,0:T(8,128)}), f32[3,512,512]{2,1,0:T(8,128)}) %all-reduce.2.cloned.1.call-update) | async-done | bytes 3145744 | tf_op jit(solution)/shard_map/psum | solution.py:48
  931.2 4.3 sub.3
  (36 shorter events, 4.0 us)
Async XLA Ops:
  7.2 360.5 %reduce-scatter.8.cloned.1.call-start = ((), (), s32[]{:S(2)}) async-start(), calls=%async_computation.8 | async-start | bytes 14155776 | tf_op jit(solution)/shard_map/reduce_scatter | solution.py:10
  11.4 0.9 copy-start.7
  11.4 0.9 collective-permute-start.2
  101.5 1.1 copy-start.6
  101.6 476.2 %reduce-scatter.4.cloned.1.call-start = ((), (), s32[]{:S(2)}) async-start(), calls=%async_computation.6 | async-start | bytes 14155776 | tf_op jit(solution)/shard_map/reduce_scatter | solution.py:10
  102.7 0.7 collective-permute-start
  225.7 1.1 copy-start.4
  225.7 562.3 %reduce-scatter.6.cloned.1.call-start = ((), (), s32[]{:S(2)}) async-start(), calls=%async_computation.7 | async-start | bytes 14155776 | tf_op jit(solution)/shard_map/reduce_scatter | solution.py:10
  226.8 0.7 collective-permute-start.1
  367.0 1.2 copy-start.8
  367.0 421.0 %copy-start.5 = (bf16[768,512]{1,0:T(8,128)(2,1)S(1)}, bf16[768,512]{1,0:T(8,128)(2,1)}, u32[]{:S(2)}) copy-start(bf16[768,512]{1,0:T(8,128)(2,1)} %get-tuple-element.9) | copy-start | bytes 2359300
  367.0 564.2 %all-reduce.2.cloned.1.call-start = ((), (), s32[]{:S(2)}) async-start(), calls=%async_computation.9 | async-start | bytes 6291456 | tf_op jit(solution)/shard_map/psum | solution.py:48
  793.1 1.4 copy-start
  793.1 1.9 copy-start.2
  794.5 1.5 copy-start.1
  798.6 132.6 %copy-start.3 = (f32[3,512,512]{2,1,0:T(8,128)S(1)}, f32[3,512,512]{2,1,0:T(8,128)}, u32[]{:S(2)}) copy-start(f32[3,512,512]{2,1,0:T(8,128)} %param.6) | copy-start | bytes 9437188
Sparse Core Ops, SparseCore 0:
  101.7 265.9 reduce-scatter.7
  371.2 206.5 reduce-scatter.3
  581.4 206.5 reduce-scatter.5
  793.9 137.2 all-reduce.1
